TPU v7x, 256 devices: a whole 4x4x8 slice. The times are simulated.
256 devices in a mesh: row: 16 (over y_hi, z), col: 16 (over x, y_lo, core).
Axes of the slice: x: 4, y: 4 (y_hi: 2, y_lo: 2; y = y_hi * 2 + y_lo), z: 8, core: 2. Of those that a mesh axis runs over, the one named last changes fastest.
Arguments:
- fields: float32 [1, 4, 256, 256, 256], P(None, None, 'row', 'col'), may hold values from -6 to 6
- cotangent: float32 [1, 4, 256, 256, 256], P(None, None, 'row', 'col'), may hold values from -6 to 6
- spec_weights: float32 [2, 4, 4, 16, 16, 16], replicated, may hold values from -96 to 96
- point_weights: float32 [4, 4], replicated, may hold values from -3 to 3
- bias: float32 [4], replicated, may hold values from -3 to 3
Outputs:
- grad_fields: float32 [1, 4, 256, 256, 256], P(None, None, 'row', 'col')
- grad_spectral: float32 [2, 4, 4, 16, 16, 16], replicated
All inputs are finite; a program needn't handle non-finite values.
Results may differ from a plain program's by a relative error of at most 0.00011.
Values sent between devices are 32-bit elements; how exact they have to be, the bound alone decides.
A program may use at most 64 MiB of HBM per device.

v0:
```python
import math
import jax
import jax.numpy as jnp
from jax import lax
from jax.sharding import PartitionSpec as P

C = 4
NX = 256
NY = 256
NZ = 256
MX = 16
MY = 16
MZ = 16
highest = lax.Precision.HIGHEST


def phase_tables(number, length, signed, start, count):
    wavenum = jnp.arange(number, dtype=jnp.int32)
    if signed:
        wavenum = jnp.where(wavenum < number // 2, wavenum, wavenum + length - number)
    points = start + jnp.arange(count, dtype=jnp.int32)
    angles = (
        2.0 * math.pi / length * (points[:, None] * wavenum[None, :] % length).astype(jnp.float32)
    )
    return (jnp.cos(angles), jnp.sin(angles))


def forward_table(number, length, start, count):
    cosine, sine = phase_tables(number, length, True, start, count)
    return jnp.stack([jnp.stack([cosine, -sine], 1), jnp.stack([sine, cosine], 1)], 0)


def inverse_table(number, length, start, count):
    cosine, sine = phase_tables(number, length, True, start, count)
    cosine = cosine.T
    sine = sine.T
    return jnp.stack([jnp.stack([cosine, sine], 1), jnp.stack([-sine, cosine], 1)], 0)


def first_table():
    cos_x, sin_x = phase_tables(MX, NX, False, 0, NX)
    return jnp.stack([cos_x, -sin_x], 1)


def last_table():
    cos_x, sin_x = phase_tables(MX, NX, False, 0, NX)
    wavenum = jnp.arange(MX, dtype=jnp.int32)
    weighting = jnp.where(wavenum == 0, 1.0, 2.0).astype(jnp.float32) / float(NX * NY * NZ)
    return jnp.stack([cos_x.T * weighting[:, None], -sin_x.T * weighting[:, None]], 0)


def to_modes(field):
    along_x = jnp.einsum("bcyzx,xtp->btpczy", field, first_table(), precision=highest)
    gathered = lax.all_to_all(along_x, "row", split_axis=2, concat_axis=5, tiled=True)
    along_y = jnp.einsum(
        "bspczy,sytq->btpcqz", gathered, forward_table(MY, NY, 0, NY), precision=highest
    )
    swapped = lax.all_to_all(along_y, "col", split_axis=4, concat_axis=5, tiled=True)
    return jnp.einsum(
        "bspcqz,sztr->btpcqr", swapped, forward_table(MZ, NZ, 0, NZ), precision=highest
    )


def from_modes(modes):
    along_z = jnp.einsum(
        "bspcqr,srtz->btpcqz", modes, inverse_table(MZ, NZ, 0, NZ), precision=highest
    )
    swapped = lax.all_to_all(along_z, "col", split_axis=5, concat_axis=4, tiled=True)
    along_y = jnp.einsum(
        "bspcqz,sqty->btpczy", swapped, inverse_table(MY, NY, 0, NY), precision=highest
    )
    gathered = lax.all_to_all(along_y, "row", split_axis=5, concat_axis=2, tiled=True)
    return jnp.einsum("btpczy,tpx->bcyzx", gathered, last_table(), precision=highest)


def per_device(fields, cotangent, spec_weights, point_weights, bias):
    row_pos = lax.axis_index("row")
    col_pos = lax.axis_index("col")
    zero_index = jnp.zeros((), jnp.int32)
    kx_local = MX // lax.axis_size("row")
    ky_local = MY // lax.axis_size("col")
    starts = (
        zero_index,
        zero_index,
        zero_index,
        row_pos * kx_local,
        col_pos * ky_local,
        zero_index,
    )
    owned_weights = lax.dynamic_slice(spec_weights, starts, (2, C, C, kx_local, ky_local, MZ))
    kx_start = row_pos * kx_local
    weight_real = owned_weights[0]
    weight_imag = owned_weights[1]
    spectrum_u = to_modes(fields)
    input_real = spectrum_u[:, 0]
    input_imag = spectrum_u[:, 1]
    mix_form = "bpiqr,iopqr->bpoqr"
    mixed_real = jnp.einsum(mix_form, input_real, weight_real, precision=highest) - jnp.einsum(
        mix_form, input_imag, weight_imag, precision=highest
    )
    mixed_imag = jnp.einsum(mix_form, input_real, weight_imag, precision=highest) + jnp.einsum(
        mix_form, input_imag, weight_real, precision=highest
    )
    spectral_term = from_modes(jnp.stack([mixed_real, mixed_imag], 1))
    local_term = jnp.einsum("bcyzx,co->boyzx", fields, point_weights, precision=highest)
    pre_activation = spectral_term + local_term + bias[None, :, None, None, None]
    gelu_slope = 0.5 * (1.0 + lax.erf(pre_activation / math.sqrt(2.0))) + pre_activation * jnp.exp(
        -0.5 * pre_activation * pre_activation
    ) / math.sqrt(2.0 * math.pi)
    upstream = cotangent * gelu_slope
    spectrum_h = to_modes(upstream)
    back_real = spectrum_h[:, 0]
    back_imag = spectrum_h[:, 1]
    grad_form = "bpiqr,bpoqr->iopqr"
    grad_real = jnp.einsum(grad_form, input_real, back_real, precision=highest) + jnp.einsum(
        grad_form, input_imag, back_imag, precision=highest
    )
    grad_imag = jnp.einsum(grad_form, input_real, back_imag, precision=highest) - jnp.einsum(
        grad_form, input_imag, back_real, precision=highest
    )
    wave_global = kx_start + jnp.arange(kx_local, dtype=jnp.int32)
    factor = jnp.where(wave_global == 0, 1.0, 2.0).astype(jnp.float32) / float(NX * NY * NZ)
    grad_block = jnp.stack([grad_real, grad_imag], 0) * factor[None, None, None, :, None, None]
    adj_form = "iopqr,bpoqr->bpiqr"
    adjoint_real = jnp.einsum(adj_form, weight_real, back_real, precision=highest) + jnp.einsum(
        adj_form, weight_imag, back_imag, precision=highest
    )
    adjoint_imag = jnp.einsum(adj_form, weight_real, back_imag, precision=highest) - jnp.einsum(
        adj_form, weight_imag, back_real, precision=highest
    )
    grad_fields = from_modes(jnp.stack([adjoint_real, adjoint_imag], 1))
    grad_fields = grad_fields + jnp.einsum(
        "boyzx,co->bcyzx", upstream, point_weights, precision=highest
    )
    full_grad = jnp.zeros((2, C, C, MX, MY, MZ), jnp.float32)
    full_grad = lax.dynamic_update_slice(full_grad, grad_block, starts)
    grad_spectral = lax.psum(full_grad, ("row", "col"))
    return (grad_fields, grad_spectral)


def solution(mesh):
    placed = (P(None, None, "row", "col", None), P(None, None, "row", "col", None), P(), P(), P())
    return jax.shard_map(
        per_device,
        mesh=mesh,
        in_specs=placed,
        out_specs=(P(None, None, "row", "col", None), P()),
        check_vma=False,
    )
```

profile of v0, /device:TPU:2, one launch (start us, length us, event | category | flops | bytes accessed | tf_op | source)
XLA Modules:
  0.0 427.5 jit_solution(5578637302729846114)
XLA Ops:
  7.3 1.1 copy-done
  8.4 4.4 %convolution_bitcast_fusion.3 = f32[1,2,16,4,16,16]{4,2,5,3,1,0:T(8,128)S(1)} fusion(f32[1,4,16,16,256]{4,3,2,1,0:T(8,128)S(1)} %copy-done, f32[256,1,16]{0,2,1:T(8,128)S(1)} %get-tuple-element.46, f32[256,1,16]{0,2,1:T(8,128)S(1)} %get-tuple-element.47), kind=kOutput, calls=%fused_computation.7 | convolution fusion | flops 100671488 | bytes 1212416 | tf_op jit(solution)/shard_map/bcyzx,xtp->btpczy/dot_general | solution.py:53
  13.2 1.0 reshape.708
  14.2 11.2 %all-to-all-start = ((f32[16,1,2048]{2,1,0:T(1,128)}), f32[16,1,2048]{2,1,0:T(1,128)S(1)}, u32[]{:S(2)}, u32[]{:S(2)}) async-start(f32[16,1,2048]{2,1,0:T(1,128)} %reshape.708), calls=%async_computation | async-start | bytes 262144 | tf_op jit(solution)/shard_map/all_to_all | solution.py:54
  25.8 9.7 %all-to-all-done = f32[16,1,2048]{2,1,0:T(1,128)S(1)} async-done(((f32[16,1,2048]{2,1,0:T(1,128)}), f32[16,1,2048]{2,1,0:T(1,128)S(1)}, u32[]{:S(2)}, u32[]{:S(2)}) %all-to-all-start) | async-done | bytes 131104 | tf_op jit(solution)/shard_map/all_to_all | solution.py:54
  36.0 0.9 reduce.16
  38.4 0.7 convolution_bitcast_fusion.7
  39.1 0.7 reshape.710
  39.8 5.0 %all-to-all-start.1 = ((f32[16,1,128]{2,1,0:T(1,128)}), f32[16,1,128]{2,1,0:T(1,128)S(1)}, u32[]{:S(2)}, u32[]{:S(2)}) async-start(f32[16,1,128]{2,1,0:T(1,128)} %reshape.710), calls=%async_computation.1 | async-start | bytes 16384 | tf_op jit(solution)/shard_map/all_to_all | solution.py:58
  44.7 0.9 constant_dynamic-slice_fusion.1
  45.6 3.8 all-to-all-done.1
  49.4 0.6 reduce.17
  51.0 1.0 reshape.712
  52.0 4.7 %all-to-all-start.2 = ((f32[16,1,128]{2,1,0:T(1,128)}), f32[16,1,128]{2,1,0:T(1,128)S(1)}, u32[]{:S(2)}, u32[]{:S(2)}) async-start(f32[16,1,128]{2,1,0:T(1,128)} %reshape.712), calls=%async_computation.2 | async-start | bytes 16384 | tf_op jit(solution)/shard_map/all_to_all | solution.py:68
  56.8 2.8 fusion.16
  59.6 1.9 all-to-all-done.2
  61.5 0.6 reduce.18
  63.6 1.5 reshape.714
  65.1 3.9 all-to-all-start.3
  69.1 10.0 %all-to-all-done.3 = f32[16,1,2048]{2,1,0:T(1,128)S(1)} async-done(((f32[16,1,2048]{2,1,0:T(1,128)}), f32[16,1,2048]{2,1,0:T(1,128)S(1)}, u32[]{:S(2)}, u32[]{:S(2)}) %all-to-all-start.3) | async-done | bytes 131104 | tf_op jit(solution)/shard_map/all_to_all | solution.py:72
  79.1 0.9 reduce.19
  80.0 0.7 reshape.715
  80.7 2.2 copy.86
  82.9 4.0 fusion.8
  86.9 4.3 convolution_bitcast_fusion.1
  91.9 13.1 %all_to_all.96 = f32[16,1,2048]{2,1,0:T(1,128)S(1)} all-to-all(f32[16,1,2048]{2,1,0:T(1,128)S(1)} %reshape.716), channel_id=1, replica_groups=mesh['row'=16,'col'=16] {'row'}, dimensions={0} | all-to-all | bytes 262144 | tf_op jit(solution)/shard_map/all_to_all | solution.py:54
  105.1 0.9 reduce.20
  106.4 1.1 bitcast_bitcast_fusion
  107.4 1.7 copy.188
  109.5 0.7 convolution_bitcast_fusion.6
  110.3 8.6 %all_to_all.97 = f32[16,1,128]{2,1,0:T(1,128)S(1)} all-to-all(f32[16,1,128]{2,1,0:T(1,128)S(1)} %reshape.718), channel_id=1, replica_groups=mesh['row'=16,'col'=16] {'col'}, dimensions={0} | all-to-all | bytes 16384 | tf_op jit(solution)/shard_map/all_to_all | solution.py:58
  119.0 0.6 reduce.21
  120.7 1.0 reshape.720
  121.6 4.7 %all-to-all-start.6 = ((f32[16,1,128]{2,1,0:T(1,128)}), f32[16,1,128]{2,1,0:T(1,128)S(1)}, u32[]{:S(2)}, u32[]{:S(2)}) async-start(f32[16,1,128]{2,1,0:T(1,128)} %reshape.720), calls=%async_computation.6 | async-start | bytes 16384 | tf_op jit(solution)/shard_map/all_to_all | solution.py:68
  126.3 4.7 %all-to-all-done.6 = f32[16,1,128]{2,1,0:T(1,128)S(1)} async-done(((f32[16,1,128]{2,1,0:T(1,128)}), f32[16,1,128]{2,1,0:T(1,128)S(1)}, u32[]{:S(2)}, u32[]{:S(2)}) %all-to-all-start.6) | async-done | bytes 8224 | tf_op jit(solution)/shard_map/all_to_all | solution.py:68
  133.2 1.5 reshape.722
  134.7 3.8 all-to-all-start.7
  138.6 2.6 fusion.13
  141.2 2.5 broadcast_in_dim.14
  143.7 1.6 dynamic_update_slice.3
  145.3 3.3 all-to-all-done.7
  148.6 0.9 reduce.23
  149.5 1.7 reshape.723
  151.3 2.2 copy.103
  153.5 1.4 fusion
  154.9 1.6 copy.108
  156.5 259.6 %all-reduce.2.cloned.1.call-done = f32[2,4,4,16,16,16]{5,4,3,2,1,0:T(8,128)} async-done(((f32[2,4,4,16,16,16]{5,4,3,2,1,0:T(8,128)}), f32[2,4,4,16,16,16]{5,4,3,2,1,0:T(8,128)}) %all-reduce.2.cloned.1.call-update) | async-done | bytes 524304 | tf_op jit(solution)/shard_map/psum | solution.py:137
  416.0 4.7 %copy.228 = f32[2,4,4,16,16,16]{5,4,3,2,1,0:T(8,128)} copy(f32[2,4,4,16,16,16]{5,4,3,2,1,0:T(8,128)} %all-reduce.2.cloned.1.call-done) | data formatting | bytes 1048576
  (58 shorter events, 10.2 us)
Async XLA Ops:
  7.2 1.2 copy-start
  14.2 21.3 %all-to-all-start = ((f32[16,1,2048]{2,1,0:T(1,128)}), f32[16,1,2048]{2,1,0:T(1,128)S(1)}, u32[]{:S(2)}, u32[]{:S(2)}) async-start(f32[16,1,2048]{2,1,0:T(1,128)} %reshape.708), calls=%async_computation | async-start | bytes 262144 | tf_op jit(solution)/shard_map/all_to_all | solution.py:54
  36.0 20.7 %copy-start.1 = (f32[4,4]{1,0:T(4,128)S(1)}, f32[4,4]{1,0:T(4,128)}, u32[]{:S(2)}) copy-start(f32[4,4]{1,0:T(4,128)} %param.8) | copy-start | bytes 196
  39.8 9.6 %all-to-all-start.1 = ((f32[16,1,128]{2,1,0:T(1,128)}), f32[16,1,128]{2,1,0:T(1,128)S(1)}, u32[]{:S(2)}, u32[]{:S(2)}) async-start(f32[16,1,128]{2,1,0:T(1,128)} %reshape.710), calls=%async_computation.1 | async-start | bytes 16384 | tf_op jit(solution)/shard_map/all_to_all | solution.py:58
  52.0 9.5 %all-to-all-start.2 = ((f32[16,1,128]{2,1,0:T(1,128)}), f32[16,1,128]{2,1,0:T(1,128)S(1)}, u32[]{:S(2)}, u32[]{:S(2)}) async-start(f32[16,1,128]{2,1,0:T(1,128)} %reshape.712), calls=%async_computation.2 | async-start | bytes 16384 | tf_op jit(solution)/shard_map/all_to_all | solution.py:68
  56.8 26.1 %copy-start.2 = (f32[4]{0:T(128)S(1)}, f32[4]{0:T(128)}, u32[]{:S(2)}) copy-start(f32[4]{0:T(128)} %param.9) | copy-start | bytes 52
  65.1 13.9 %all-to-all-start.3 = ((f32[16,1,2048]{2,1,0:T(1,128)}), f32[16,1,2048]{2,1,0:T(1,128)S(1)}, u32[]{:S(2)}, u32[]{:S(2)}) async-start(f32[16,1,2048]{2,1,0:T(1,128)} %reshape.714), calls=%async_computation.3 | async-start | bytes 262144 | tf_op jit(solution)/shard_map/all_to_all | solution.py:72
  121.6 9.4 %all-to-all-start.6 = ((f32[16,1,128]{2,1,0:T(1,128)}), f32[16,1,128]{2,1,0:T(1,128)S(1)}, u32[]{:S(2)}, u32[]{:S(2)}) async-start(f32[16,1,128]{2,1,0:T(1,128)} %reshape.720), calls=%async_computation.6 | async-start | bytes 16384 | tf_op jit(solution)/shard_map/all_to_all | solution.py:68
  134.7 13.9 %all-to-all-start.7 = ((f32[16,1,2048]{2,1,0:T(1,128)}), f32[16,1,2048]{2,1,0:T(1,128)S(1)}, u32[]{:S(2)}, u32[]{:S(2)}) async-start(f32[16,1,2048]{2,1,0:T(1,128)} %reshape.722), calls=%async_computation.7 | async-start | bytes 262144 | tf_op jit(solution)/shard_map/all_to_all | solution.py:72
  138.5 277.5 %all-reduce.2.cloned.1.call-start = ((), (), s32[]{:S(2)}) async-start(), calls=%async_computation.8 | async-start | bytes 8388608 | tf_op jit(solution)/shard_map/psum | solution.py:137
Sparse Core Ops, SparseCore 0:
  145.4 270.5 all-reduce.1
where the time goes:
time: 428 us
  waiting for transfers between devices  293 us (68%)
  local copies, waits for them, and re-layouts  35.6 us (8%)
  starting transfers between devices  33.4 us (8%)
  matrix products  22.5 us (5%)
  blocking collectives  21.8 us (5%)
  between operations  14.5 us (3%)
  other arithmetic  6.94 us (2%)
    psum x1, waiting for transfers between devices, per_device(): grad_spectral = lax.psum(full_grad, ('row', 'col'))  260 us
    unnamed x26, local copies, waits for them, and re-layouts  18.6 us
    all_to_all x2, waiting for transfers between devices, from_modes(): lax.all_to_all(along_y, 'row', split_axis=5, concat_axis=2, tiled=True)  13.3 us
    all_to_all x1, blocking collectives, to_modes(): lax.all_to_all(along_x, 'row', split_axis=2, concat_axis=5, tiled=True)  13.1 us
    all_to_all x1, starting transfers between devices, to_modes(): lax.all_to_all(along_x, 'row', split_axis=2, concat_axis=5, tiled=True)  11.2 us
    all_to_all x1, waiting for transfers between devices, to_modes(): lax.all_to_all(along_x, 'row', split_axis=2, concat_axis=5, tiled=True)  9.72 us
    all_to_all x2, starting transfers between devices, from_modes(): lax.all_to_all(along_z, 'col', split_axis=5, concat_axis=4, tiled=True)  9.46 us
    dot_general x2, matrix products, to_modes(): jnp.einsum('bcyzx,xtp->btpczy', field, first_table(), precision=highest)  8.67 us
  transfers between devices with their start and end apart: 7, of which 7 were waited for; matrix products, arithmetic and copies ran while one was open for 4% of the time, Pallas kernels for 0%

commit v1 on v0

--- a/solution.py
+++ b/solution.py
@@ -134,7 +134,8 @@
     )
     full_grad = jnp.zeros((2, C, C, MX, MY, MZ), jnp.float32)
     full_grad = lax.dynamic_update_slice(full_grad, grad_block, starts)
-    grad_spectral = lax.psum(full_grad, ("row", "col"))
+    one_axis = lax.psum(full_grad, "col")
+    grad_spectral = lax.psum(one_axis, "row")
     return (grad_fields, grad_spectral)
 
 

time: 428 us -> 446 us (1.042)
  waiting for transfers between devices: 293 us -> 311 us
    psum x1 -> x2, waiting for transfers between devices: 260 us -> 281 us  [the longest x1 172 us: per_device(): grad_spectral = lax.psum(one_axis, 'row')]
    all_to_all x2 -> x1, starting transfers between devices: 9.46 us -> 4.74 us  [from_modes(): lax.all_to_all(along_z, 'col', split_axis=5, concat_axis=4, tiled=True)]
    all_to_all x1 -> x2, starting transfers between devices: 4.96 us -> 9.68 us  [to_modes(): lax.all_to_all(along_y, 'col', split_axis=4, concat_axis=5, tiled=True)]
    all_to_all x2 -> x1, waiting for transfers between devices: 6.58 us -> 1.87 us  [from_modes(): lax.all_to_all(along_z, 'col', split_axis=5, concat_axis=4, tiled=True)]
    all_to_all x1 -> x2, waiting for transfers between devices: 3.75 us -> 8.41 us  [to_modes(): lax.all_to_all(along_y, 'col', split_axis=4, concat_axis=5, tiled=True)]
  transfers between devices with their start and end apart: 7 -> 8, of which waited for: 7 -> 7; matrix products, arithmetic and copies ran while one was open for 4% -> 4% of each run, Pallas kernels for 0% -> 0%
where the time goes in v1:
time: 446 us; the launch traced here: 445 us
  waiting for transfers between devices  311 us (70%)
  local copies, waits for them, and re-layouts  35.6 us (8%)
  starting transfers between devices  33.1 us (7%)
  matrix products  22.5 us (5%)
  blocking collectives  22 us (5%)
  between operations  14.5 us (3%)
  other arithmetic  6.56 us (1%)
    psum x1, waiting for transfers between devices, per_device(): grad_spectral = lax.psum(one_axis, 'row')  172 us
    psum x1, waiting for transfers between devices, per_device(): one_axis = lax.psum(full_grad, 'col')  108 us
    unnamed x26, local copies, waits for them, and re-layouts  18.6 us
    all_to_all x1, blocking collectives, to_modes(): lax.all_to_all(along_x, 'row', split_axis=2, concat_axis=5, tiled=True)  13.1 us
    all_to_all x1, starting transfers between devices, to_modes(): lax.all_to_all(along_x, 'row', split_axis=2, concat_axis=5, tiled=True)  11.2 us
    all_to_all x2, waiting for transfers between devices, from_modes(): lax.all_to_all(along_y, 'row', split_axis=5, concat_axis=2, tiled=True)  9.97 us
    all_to_all x1, waiting for transfers between devices, to_modes(): lax.all_to_all(along_x, 'row', split_axis=2, concat_axis=5, tiled=True)  9.72 us
    all_to_all x2, starting transfers between devices, to_modes(): lax.all_to_all(along_y, 'col', split_axis=4, concat_axis=5, tiled=True)  9.68 us
  transfers between devices with their start and end apart: 8, of which 7 were waited for; matrix products, arithmetic and copies ran while one was open for 4% of the time, Pallas kernels for 0%

profile of v1, /device:TPU:2, one launch (start us, length us, event | category | flops | bytes accessed | tf_op | source)
XLA Modules:
  0.0 444.9 jit_solution(5522735286655537487)
XLA Ops:
  7.3 1.1 copy-done
  8.4 4.4 convolution_bitcast_fusion.3
  13.2 1.0 reshape.708
  14.2 11.2 %all-to-all-start = ((f32[16,1,2048]{2,1,0:T(1,128)}), f32[16,1,2048]{2,1,0:T(1,128)S(1)}, u32[]{:S(2)}, u32[]{:S(2)}) async-start(f32[16,1,2048]{2,1,0:T(1,128)} %reshape.708), calls=%async_computation | async-start | bytes 262144 | tf_op jit(solution)/shard_map/all_to_all | solution.py:54
  25.8 9.7 %all-to-all-done = f32[16,1,2048]{2,1,0:T(1,128)S(1)} async-done(((f32[16,1,2048]{2,1,0:T(1,128)}), f32[16,1,2048]{2,1,0:T(1,128)S(1)}, u32[]{:S(2)}, u32[]{:S(2)}) %all-to-all-start) | async-done | bytes 131104 | tf_op jit(solution)/shard_map/all_to_all | solution.py:54
  36.0 0.9 reduce.16
  38.3 0.7 convolution_bitcast_fusion.7
  39.0 0.7 reshape.710
  39.7 5.0 %all-to-all-start.1 = ((f32[16,1,128]{2,1,0:T(1,128)}), f32[16,1,128]{2,1,0:T(1,128)S(1)}, u32[]{:S(2)}, u32[]{:S(2)}) async-start(f32[16,1,128]{2,1,0:T(1,128)} %reshape.710), calls=%async_computation.1 | async-start | bytes 16384 | tf_op jit(solution)/shard_map/all_to_all | solution.py:58
  44.6 0.9 constant_dynamic-slice_fusion.1
  45.5 3.8 all-to-all-done.1
  49.3 0.6 reduce.17
  50.9 1.0 reshape.712
  51.9 4.7 %all-to-all-start.2 = ((f32[16,1,128]{2,1,0:T(1,128)}), f32[16,1,128]{2,1,0:T(1,128)S(1)}, u32[]{:S(2)}, u32[]{:S(2)}) async-start(f32[16,1,128]{2,1,0:T(1,128)} %reshape.712), calls=%async_computation.2 | async-start | bytes 16384 | tf_op jit(solution)/shard_map/all_to_all | solution.py:68
  56.6 2.8 fusion.16
  59.4 1.9 all-to-all-done.2
  61.3 0.6 reduce.18
  63.5 1.5 reshape.714
  64.9 3.9 all-to-all-start.3
  68.9 10.0 %all-to-all-done.3 = f32[16,1,2048]{2,1,0:T(1,128)S(1)} async-done(((f32[16,1,2048]{2,1,0:T(1,128)}), f32[16,1,2048]{2,1,0:T(1,128)S(1)}, u32[]{:S(2)}, u32[]{:S(2)}) %all-to-all-start.3) | async-done | bytes 131104 | tf_op jit(solution)/shard_map/all_to_all | solution.py:72
  78.9 0.9 reduce.19
  79.8 0.7 reshape.715
  80.5 2.2 copy.86
  82.7 4.0 fusion.8
  86.7 4.3 convolution_bitcast_fusion.1
  91.7 13.1 %all_to_all.96 = f32[16,1,2048]{2,1,0:T(1,128)S(1)} all-to-all(f32[16,1,2048]{2,1,0:T(1,128)S(1)} %reshape.716), channel_id=1, replica_groups=mesh['row'=16,'col'=16] {'row'}, dimensions={0} | all-to-all | bytes 262144 | tf_op jit(solution)/shard_map/all_to_all | solution.py:54
  104.8 0.9 reduce.20
  106.1 1.1 bitcast_bitcast_fusion
  107.1 1.7 copy.188
  109.3 0.7 convolution_bitcast_fusion.6
  110.0 0.7 reshape.718
  110.7 4.7 %all-to-all-start.5 = ((f32[16,1,128]{2,1,0:T(1,128)}), f32[16,1,128]{2,1,0:T(1,128)S(1)}, u32[]{:S(2)}, u32[]{:S(2)}) async-start(f32[16,1,128]{2,1,0:T(1,128)} %reshape.718), calls=%async_computation.5 | async-start | bytes 16384 | tf_op jit(solution)/shard_map/all_to_all | solution.py:58
  115.4 4.7 %all-to-all-done.5 = f32[16,1,128]{2,1,0:T(1,128)S(1)} async-done(((f32[16,1,128]{2,1,0:T(1,128)}), f32[16,1,128]{2,1,0:T(1,128)S(1)}, u32[]{:S(2)}, u32[]{:S(2)}) %all-to-all-start.5) | async-done | bytes 8224 | tf_op jit(solution)/shard_map/all_to_all | solution.py:58
  121.3 2.5 broadcast_in_dim.14
  123.8 1.6 dynamic_update_slice.3
  126.2 8.9 %all_to_all.97 = f32[16,1,128]{2,1,0:T(1,128)S(1)} all-to-all(f32[16,1,128]{2,1,0:T(1,128)S(1)} %reshape.720), channel_id=1, replica_groups=mesh['row'=16,'col'=16] {'col'}, dimensions={0} | all-to-all | bytes 16384 | tf_op jit(solution)/shard_map/all_to_all | solution.py:68
  135.1 0.6 reduce.22
  137.3 1.5 reshape.722
  138.8 3.5 all-to-all-start.7
  142.3 108.4 %all-reduce.3.cloned.1.call-done = f32[2,4,4,16,16,16]{5,4,3,2,1,0:T(8,128)} async-done(((f32[2,4,4,16,16,16]{5,4,3,2,1,0:T(8,128)}), f32[2,4,4,16,16,16]{5,4,3,2,1,0:T(8,128)}) %all-reduce.3.cloned.1.call-update) | async-done | bytes 524304 | tf_op jit(solution)/shard_map/psum | solution.py:137
  250.8 2.6 fusion.13
  253.3 0.9 reduce.23
  254.2 1.7 reshape.723
  255.9 2.2 copy.103
  258.1 1.4 fusion
  259.6 1.6 copy.108
  261.1 172.3 %all-reduce.5.cloned.1.call-done = f32[2,4,4,16,16,16]{5,4,3,2,1,0:T(8,128)} async-done(((f32[2,4,4,16,16,16]{5,4,3,2,1,0:T(8,128)}), f32[2,4,4,16,16,16]{5,4,3,2,1,0:T(8,128)}) %all-reduce.5.cloned.1.call-update) | async-done | bytes 524304 | tf_op jit(solution)/shard_map/psum | solution.py:138
  433.4 4.7 %copy.229 = f32[2,4,4,16,16,16]{5,4,3,2,1,0:T(8,128)} copy(f32[2,4,4,16,16,16]{5,4,3,2,1,0:T(8,128)} %all-reduce.5.cloned.1.call-done) | data formatting | bytes 1048576
  (61 shorter events, 10.4 us)
Async XLA Ops:
  7.2 1.2 copy-start
  14.2 21.3 %all-to-all-start = ((f32[16,1,2048]{2,1,0:T(1,128)}), f32[16,1,2048]{2,1,0:T(1,128)S(1)}, u32[]{:S(2)}, u32[]{:S(2)}) async-start(f32[16,1,2048]{2,1,0:T(1,128)} %reshape.708), calls=%async_computation | async-start | bytes 262144 | tf_op jit(solution)/shard_map/all_to_all | solution.py:54
  36.0 20.6 %copy-start.1 = (f32[4,4]{1,0:T(4,128)S(1)}, f32[4,4]{1,0:T(4,128)}, u32[]{:S(2)}) copy-start(f32[4,4]{1,0:T(4,128)} %param.8) | copy-start | bytes 196
  39.7 9.6 %all-to-all-start.1 = ((f32[16,1,128]{2,1,0:T(1,128)}), f32[16,1,128]{2,1,0:T(1,128)S(1)}, u32[]{:S(2)}, u32[]{:S(2)}) async-start(f32[16,1,128]{2,1,0:T(1,128)} %reshape.710), calls=%async_computation.1 | async-start | bytes 16384 | tf_op jit(solution)/shard_map/all_to_all | solution.py:58
  51.9 9.5 %all-to-all-start.2 = ((f32[16,1,128]{2,1,0:T(1,128)}), f32[16,1,128]{2,1,0:T(1,128)S(1)}, u32[]{:S(2)}, u32[]{:S(2)}) async-start(f32[16,1,128]{2,1,0:T(1,128)} %reshape.712), calls=%async_computation.2 | async-start | bytes 16384 | tf_op jit(solution)/shard_map/all_to_all | solution.py:68
  56.6 26.0 %copy-start.2 = (f32[4]{0:T(128)S(1)}, f32[4]{0:T(128)}, u32[]{:S(2)}) copy-start(f32[4]{0:T(128)} %param.9) | copy-start | bytes 52
  64.9 13.9 %all-to-all-start.3 = ((f32[16,1,2048]{2,1,0:T(1,128)}), f32[16,1,2048]{2,1,0:T(1,128)S(1)}, u32[]{:S(2)}, u32[]{:S(2)}) async-start(f32[16,1,2048]{2,1,0:T(1,128)} %reshape.714), calls=%async_computation.3 | async-start | bytes 262144 | tf_op jit(solution)/shard_map/all_to_all | solution.py:72
  110.7 9.4 %all-to-all-start.5 = ((f32[16,1,128]{2,1,0:T(1,128)}), f32[16,1,128]{2,1,0:T(1,128)S(1)}, u32[]{:S(2)}, u32[]{:S(2)}) async-start(f32[16,1,128]{2,1,0:T(1,128)} %reshape.718), calls=%async_computation.5 | async-start | bytes 16384 | tf_op jit(solution)/shard_map/all_to_all | solution.py:58
  115.4 135.3 %all-reduce.3.cloned.1.call-start = ((), (), s32[]{:S(2)}) async-start(), calls=%async_computation.8 | async-start | bytes 8388608 | tf_op jit(solution)/shard_map/psum | solution.py:137
  138.8 114.6 %all-to-all-start.7 = ((f32[16,1,2048]{2,1,0:T(1,128)}), f32[16,1,2048]{2,1,0:T(1,128)S(1)}, u32[]{:S(2)}, u32[]{:S(2)}) async-start(f32[16,1,2048]{2,1,0:T(1,128)} %reshape.722), calls=%async_computation.7 | async-start | bytes 262144 | tf_op jit(solution)/shard_map/all_to_all | solution.py:72
  142.3 291.2 %all-reduce.5.cloned.1.call-start = ((), (), s32[]{:S(2)}) async-start(), calls=%async_computation.9 | async-start | bytes 8388608 | tf_op jit(solution)/shard_map/psum | solution.py:138
Sparse Core Ops, SparseCore 0:
  125.6 125.1 all-reduce.2
  253.4 179.9 all-reduce.4
